TPU v7x, 32 devices: a whole 2x2x4 slice. The times are simulated.
32 devices in a mesh: seqa: 4 (over z), seqb: 2 (over x), dp: 4 (over y, core).
Axes of the slice: x: 2, y: 2, z: 4, core: 2. Of those that a mesh axis runs over, the one named last changes fastest.
Arguments:
- queries: bfloat16 [1024, 8, 64], P(('dp', 'seqa', 'seqb')), parts along dimension 0, may hold values from -6 to 6
- keys: bfloat16 [1024, 8, 64], P(('dp', 'seqa', 'seqb')), parts along dimension 0, may hold values from -6 to 6
- values: bfloat16 [1024, 8, 64], P(('dp', 'seqa', 'seqb')), parts along dimension 0, may hold values from -6 to 6
- doc_bounds: int32 [36], P('dp'), parts along dimension 0, may hold values from 0 to 256, as said below
- q_gain: float32 [64], replicated, may hold values from 0.25 to 1.75
- k_gain: float32 [64], replicated, may hold values from 0.25 to 1.75
Outputs:
- attended: bfloat16 [1024, 8, 64], P(('dp', 'seqa', 'seqb')), parts along dimension 0
There are 4 independent parts, one for each index of `dp`. A program takes and returns all parts, laid end to end along the dimension named above; an argument that names none is the same for every part. Nothing has to cross between parts.
Inputs may be any that keep to these rules, and one draw needn't show every extreme that they name: doc_bounds[0] is 0, doc_bounds[8] is 256, and the entries rise strictly.
All inputs are finite; a program needn't handle non-finite values.
Results may differ from a plain program's by a relative error of at most 0.0015.
Values may be sent and summed in bfloat16 or wider, within the bound.
A program may use at most 64 MiB of HBM per device.

v0:
```python
import jax
import jax.numpy as jnp
from jax import lax
from jax.sharding import PartitionSpec as P

TOK_DEV = 32
DOCS = 8


def for_sending(value):
    return jax.tree.map(lambda a: a.astype(jnp.bfloat16) if a.dtype == jnp.float32 else a, value)


def prepare(block, gain, positions):
    values32 = block.astype(jnp.float32)
    scale = lax.rsqrt(jnp.mean(values32 * values32, axis=-1, keepdims=True) + 1e-06)
    normed = values32 * scale * gain
    half = normed.shape[-1] // 2
    freq = jnp.exp(-jnp.log(10000.0) * jnp.arange(half, dtype=jnp.float32) * 2.0 / normed.shape[-1])
    angle = positions.astype(jnp.float32)[:, None] * freq[None, :]
    first = normed[:, :half]
    second = normed[:, half:]
    cosine = jnp.cos(angle)
    sine = jnp.sin(angle)
    rotated = jnp.concatenate(
        [first * cosine - second * sine, first * sine + second * cosine], axis=-1
    )
    return rotated.astype(jnp.bfloat16)


def attend_head(query_head, key_head, value_head, doc_bounds, q_gain, k_gain):
    length, width = query_head.shape
    places = jnp.arange(length, dtype=jnp.int32)
    doc = jnp.sum((places[:, None] >= doc_bounds[None, 1:DOCS]).astype(jnp.int32), axis=1).astype(
        jnp.int32
    )
    positions = places - doc_bounds[doc]
    qr = prepare(query_head, q_gain, positions)
    kr = prepare(key_head, k_gain, positions)
    block = 8 * TOK_DEV
    count = length // block

    def one_block(items):
        query_rows, query_doc, query_place = items
        scores = jnp.dot(query_rows, kr.T, preferred_element_type=jnp.float32) / jnp.sqrt(
            jnp.float32(width)
        )
        allowed = (query_doc[:, None] == doc[None, :]) & (places[None, :] <= query_place[:, None])
        scores = jnp.where(allowed, scores, jnp.float32(-1e30))
        top = jnp.max(scores, axis=1, keepdims=True)
        expo = jnp.where(allowed, jnp.exp(scores - top), jnp.float32(0.0))
        weights = (expo / jnp.sum(expo, axis=1, keepdims=True)).astype(jnp.bfloat16)
        return jnp.dot(weights, value_head, preferred_element_type=jnp.float32).astype(jnp.bfloat16)

    outputs = lax.map(
        one_block,
        (qr.reshape(count, block, width), doc.reshape(count, block), places.reshape(count, block)),
    )
    return outputs.reshape(length, width)


def body(queries, keys, values, doc_bounds, q_gain, k_gain):
    query_full, key_full, value_full = (
        lax.all_to_all(queries, ("seqa", "seqb"), split_axis=1, concat_axis=0, tiled=True),
        lax.all_to_all(keys, ("seqa", "seqb"), split_axis=1, concat_axis=0, tiled=True),
        lax.all_to_all(values, ("seqa", "seqb"), split_axis=1, concat_axis=0, tiled=True),
    )
    attend_all = jax.vmap(attend_head, in_axes=(1, 1, 1, None, None, None), out_axes=1)
    result = attend_all(query_full, key_full, value_full, doc_bounds, q_gain, k_gain)
    back = jax.tree.map(
        lambda part, own: part.astype(own.dtype),
        lax.all_to_all(
            for_sending(result), ("seqa", "seqb"), split_axis=0, concat_axis=1, tiled=True
        ),
        result,
    )
    return back


def solution(mesh):
    placed = (
        P(("dp", "seqa", "seqb"), None, None),
        P(("dp", "seqa", "seqb"), None, None),
        P(("dp", "seqa", "seqb"), None, None),
        P("dp"),
        P(),
        P(),
    )
    return jax.shard_map(
        body,
        mesh=mesh,
        in_specs=placed,
        out_specs=P(("dp", "seqa", "seqb"), None, None),
        check_vma=False,
    )
```

profile of v0, /device:TPU:0, one launch (start us, length us, event | category | flops | bytes accessed | tf_op | source)
XLA Modules:
  0.0 51.4 jit_solution(5390356876942272930)
XLA Ops:
  0.0 0.8 %copy.39 = bf16[32,8,64]{2,0,1:T(8,128)(2,1)S(1)} copy(bf16[32,8,64]{2,1,0:T(8,128)(2,1)} %param.6) | data formatting | bytes 65536 | tf_op args[0]
  0.9 0.7 %reshape.437 = bf16[8,2,1024]{2,1,0:T(2,128)(2,1)} reshape(bf16[8,32,64]{2,1,0:T(8,128)(2,1)S(1)} %bitcast.69) | data formatting | bytes 65536
  1.6 7.4 %all-to-all-start = ((bf16[8,2,1024]{2,1,0:T(2,128)(2,1)}), bf16[8,2,1024]{2,1,0:T(2,128)(2,1)S(1)}, u32[]{:S(2)}, u32[]{:S(2)}) async-start(bf16[8,2,1024]{2,1,0:T(2,128)(2,1)} %reshape.437), calls=%async_computation | async-start | bytes 65536 | tf_op jit(solution)/shard_map/all_to_all | solution.py:64
  9.0 0.7 %fusion.35 = (s32[1]{0:T(128)}, s32[1]{0:T(128)}, s32[1]{0:T(128)}, s32[1]{0:T(128)}, s32[1]{0:T(128)}, /*index=5*/s32[1]{0:T(128)}, s32[1]{0:T(128)}, s32[1]{0:T(128)}, s32[1]{0:T(128)}) fusion(s32[9]{0:T(128)S(1)} %copy-done.2), kind=kLoop, calls=%fused_computation.61 | loop fusion | bytes 72 | tf_op jit(solution)/shard_map/vmap()/gather | solution.py:37
  9.7 0.1 convert_reduce_fusion
  9.9 0.7 %reshape.439 = bf16[8,2,1024]{2,1,0:T(2,128)(2,1)} reshape(bf16[8,32,64]{2,1,0:T(8,128)(2,1)S(1)} %bitcast.70) | data formatting | bytes 65536
  10.6 0.1 copy-done.1
  10.7 0.7 %reshape.435 = bf16[8,2,1024]{2,1,0:T(2,128)(2,1)} reshape(bf16[8,32,64]{2,1,0:T(8,128)(2,1)S(1)} %bitcast.71) | data formatting | bytes 65536
  11.5 4.4 %compare_select_fusion.1 = s32[256,1]{0,1:T(1,128)S(1)} fusion(s32[]{:T(128)} %bitcast.7, s32[]{:T(128)} %bitcast.8, s32[]{:T(128)} %bitcast.9, s32[]{:T(128)} %bitcast.10, s32[]{:T(128)} %bitcast.11, s32[]{:T(128)} %bitcast.13, s32[]{:T(128)} %bitcast.12, s32[256,1]{0,1:T(1,128)S(1)} %bitcast.74), kind=kLoop, calls=%fused_computation.50 | loop fusion | flops 3840 | bytes 2076 | tf_op jit(solution)/shard_map/vmap()/gather | solution.py:37
  15.8 1.2 %fusion.32 = f32[256]{0:T(256)S(1)} fusion(pred[256]{0:T(512)(128)(4,1)S(1)} %get-tuple-element.22, pred[256]{0:T(512)(128)(4,1)S(1)} %get-tuple-element.21, s32[256]{0:T(256)S(1)} %bitcast.75, s32[]{:T(128)} %bitcast.5, s32[]{:T(128)} %bitcast.6), kind=kLoop, calls=%fused_computation.57 | loop fusion | flops 1024 | bytes 2568 | tf_op jit(solution)/shard_map/vmap()/convert_element_type | solution.py:20
  17.1 6.0 %all-to-all-start.1 = ((bf16[8,2,1024]{2,1,0:T(2,128)(2,1)}), bf16[8,2,1024]{2,1,0:T(2,128)(2,1)S(1)}, u32[]{:S(2)}, u32[]{:S(2)}) async-start(bf16[8,2,1024]{2,1,0:T(2,128)(2,1)} %reshape.439), calls=%async_computation.1 | async-start | bytes 65536 | tf_op jit(solution)/shard_map/all_to_all | solution.py:65
  23.1 0.1 reshape.438
  23.2 0.1 multiply_reduce_fusion.1
  23.6 6.2 %all-to-all-done.1 = bf16[8,2,1024]{2,1,0:T(2,128)(2,1)S(1)} async-done(((bf16[8,2,1024]{2,1,0:T(2,128)(2,1)}), bf16[8,2,1024]{2,1,0:T(2,128)(2,1)S(1)}, u32[]{:S(2)}, u32[]{:S(2)}) %all-to-all-start.1) | async-done | bytes 32800 | tf_op jit(solution)/shard_map/all_to_all | solution.py:65
  29.8 3.3 %all-to-all-start.2 = ((bf16[8,2,1024]{2,1,0:T(2,128)(2,1)}), bf16[8,2,1024]{2,1,0:T(2,128)(2,1)S(1)}, u32[]{:S(2)}, u32[]{:S(2)}) async-start(bf16[8,2,1024]{2,1,0:T(2,128)(2,1)} %reshape.435), calls=%async_computation.2 | async-start | bytes 65536 | tf_op jit(solution)/shard_map/all_to_all | solution.py:66
  33.2 0.1 reshape.440
  33.3 0.1 multiply_reduce_fusion
  33.6 0.6 %copy-done.3 = f32[64]{0:T(128)S(1)} copy-done((f32[64]{0:T(128)S(1)}, f32[64]{0:T(128)}, u32[]{:S(2)}) %copy-start.3) | copy-done | bytes 280
  34.2 0.1 fusion.20
  34.4 0.6 %fusion.29 = (bf16[256,32]{1,0:T(8,128)(2,1)S(1)}, bf16[256,32]{1,0:T(8,128)(2,1)S(1)}, bf16[256,32]{1,0:T(8,128)(2,1)S(1)}, bf16[256,32]{1,0:T(8,128)(2,1)S(1)}) fusion(f32[1,256,64]{2,1,0:T(8,128)S(1)} %get-tuple-element.51, f32[32]{0:T(128)S(1)} %multiply_exponential_fusion, f32[256]{0:T(256)S(1)} %fusion.32, f32[1,256,64]{2,1,0:T(8,128)S(1)} %get-tuple-element.52), kind=kLoop, calls=%fused_computation.40 | loop fusion | flops 139264 | bytes 197760 | tf_op jit(solution)/shard_map/vmap()/concatenate | solution.py:25
  35.0 0.3 fusion.36
  35.3 0.1 fusion.11
  35.4 4.4 %all-to-all-done.2 = bf16[8,2,1024]{2,1,0:T(2,128)(2,1)S(1)} async-done(((bf16[8,2,1024]{2,1,0:T(2,128)(2,1)}), bf16[8,2,1024]{2,1,0:T(2,128)(2,1)S(1)}, u32[]{:S(2)}, u32[]{:S(2)}) %all-to-all-start.2) | async-done | bytes 32800 | tf_op jit(solution)/shard_map/all_to_all | solution.py:66
  39.8 0.1 reshape.436
  39.9 0.2 fusion.1
  40.1 0.5 broadcast.313
  40.7 0.7 %reduce.16 = bf16[256,64]{0,1:T(8,128)(2,1)S(1)} reduce(bf16[256,1,64]{0,2,1:T(8,128)(2,1)S(1)} %fusion.1, bf16[]{:T(256)} %broadcast.313), dimensions={1}, to_apply=%copy.29.reduce_sub_computation | reduce | bytes 65538 | tf_op jit(solution)/shard_map/vmap()/transpose;vmap()/reshape;vmap()/transpose | solution.py:69
  41.3 0.1 copy.40
  41.4 0.1 reshape.441
  41.6 9.1 %all_to_all.51 = bf16[8,2,1024]{2,1,0:T(2,128)(2,1)S(1)} all-to-all(bf16[8,2,1024]{2,1,0:T(2,128)(2,1)S(1)} %reshape.441), channel_id=1, replica_groups=mesh['seqa'=4,'seqb'=2,'dp'=4] {'seqa','seqb'}, dimensions={0} | all-to-all | bytes 65536 | tf_op jit(solution)/shard_map/all_to_all | solution.py:72
  50.6 0.1 reshape.442
  50.8 0.7 %copy.30 = bf16[32,8,64]{2,1,0:T(8,128)(2,1)} copy(bf16[32,8,64]{2,0,1:T(8,128)(2,1)S(1)} %bitcast.68) | data formatting | bytes 65536 | tf_op jit(solution)/shard_map/all_to_all | solution.py:72
  (23 shorter events, 0.6 us)
Async XLA Ops:
  0.9 8.1 %copy-start.2 = (s32[9]{0:T(128)S(1)}, s32[9]{0:T(128)}, u32[]{:S(2)}) copy-start(s32[9]{0:T(128)} %param.9) | copy-start | bytes 112
  1.6 8.3 %copy-start = (bf16[32,8,64]{2,1,0:T(8,128)(2,1)S(1)}, bf16[32,8,64]{2,1,0:T(8,128)(2,1)}, u32[]{:S(2)}) copy-start(bf16[32,8,64]{2,1,0:T(8,128)(2,1)} %param.7) | copy-start | bytes 98308
  1.6 15.5 %all-to-all-start = ((bf16[8,2,1024]{2,1,0:T(2,128)(2,1)}), bf16[8,2,1024]{2,1,0:T(2,128)(2,1)S(1)}, u32[]{:S(2)}, u32[]{:S(2)}) async-start(bf16[8,2,1024]{2,1,0:T(2,128)(2,1)} %reshape.437), calls=%async_computation | async-start | bytes 65536 | tf_op jit(solution)/shard_map/all_to_all | solution.py:64
  9.9 0.8 %copy-start.1 = (bf16[32,8,64]{2,1,0:T(8,128)(2,1)S(1)}, bf16[32,8,64]{2,1,0:T(8,128)(2,1)}, u32[]{:S(2)}) copy-start(bf16[32,8,64]{2,1,0:T(8,128)(2,1)} %param.8) | copy-start | bytes 98308
  17.1 12.7 %all-to-all-start.1 = ((bf16[8,2,1024]{2,1,0:T(2,128)(2,1)}), bf16[8,2,1024]{2,1,0:T(2,128)(2,1)S(1)}, u32[]{:S(2)}, u32[]{:S(2)}) async-start(bf16[8,2,1024]{2,1,0:T(2,128)(2,1)} %reshape.439), calls=%async_computation.1 | async-start | bytes 65536 | tf_op jit(solution)/shard_map/all_to_all | solution.py:65
  29.8 10.0 %all-to-all-start.2 = ((bf16[8,2,1024]{2,1,0:T(2,128)(2,1)}), bf16[8,2,1024]{2,1,0:T(2,128)(2,1)S(1)}, u32[]{:S(2)}, u32[]{:S(2)}) async-start(bf16[8,2,1024]{2,1,0:T(2,128)(2,1)} %reshape.435), calls=%async_computation.2 | async-start | bytes 65536 | tf_op jit(solution)/shard_map/all_to_all | solution.py:66
  33.5 0.7 %copy-start.3 = (f32[64]{0:T(128)S(1)}, f32[64]{0:T(128)}, u32[]{:S(2)}) copy-start(f32[64]{0:T(128)} %param.11) | copy-start | bytes 772
  33.5 0.7 %copy-start.4 = (f32[64]{0:T(128)S(1)}, f32[64]{0:T(128)}, u32[]{:S(2)}) copy-start(f32[64]{0:T(128)} %param.10) | copy-start | bytes 772
where the time goes:
time: 52 us; the launch traced here: 51.4 us
  starting transfers between devices  16.8 us (32%)
  waiting for transfers between devices  10.6 us (20%)
  blocking collectives  9.06 us (17%)
  other arithmetic  7.48 us (14%)
  local copies, waits for them, and re-layouts  6.8 us (13%)
  matrix products  0.54 us (1%)
    all_to_all x1, blocking collectives, body(): lax.all_to_all(for_sending(result), ('seqa', 'seqb'), split_axis=0, conca...  9.06 us
    all_to_all x1, starting transfers between devices, body(): lax.all_to_all(queries, ('seqa', 'seqb'), split_axis=1, concat_axis=0, ti...  7.41 us
    all_to_all x1, waiting for transfers between devices, body(): lax.all_to_all(keys, ('seqa', 'seqb'), split_axis=1, concat_axis=0, tiled...  6.22 us
    all_to_all x1, starting transfers between devices, body(): lax.all_to_all(keys, ('seqa', 'seqb'), split_axis=1, concat_axis=0, tiled...  6 us
    unnamed x25, local copies, waits for them, and re-layouts  4.6 us
    gather x2, other arithmetic, attend_head(): positions = places - doc_bounds[doc]  4.39 us
    all_to_all x1, waiting for transfers between devices, body(): lax.all_to_all(values, ('seqa', 'seqb'), split_axis=1, concat_axis=0, til...  4.37 us
    all_to_all x1, starting transfers between devices, body(): lax.all_to_all(values, ('seqa', 'seqb'), split_axis=1, concat_axis=0, til...  3.34 us
  transfers between devices with their start and end apart: 3, of which 2 were waited for; matrix products, arithmetic and copies ran while one was open for 19% of the time, Pallas kernels for 0%

commit v1 on v0

--- a/solution.py
+++ b/solution.py
@@ -63,7 +63,15 @@
     query_full, key_full, value_full = (
         lax.all_to_all(queries, ("seqa", "seqb"), split_axis=1, concat_axis=0, tiled=True),
         lax.all_to_all(keys, ("seqa", "seqb"), split_axis=1, concat_axis=0, tiled=True),
-        lax.all_to_all(values, ("seqa", "seqb"), split_axis=1, concat_axis=0, tiled=True),
+        jnp.concatenate(
+            lax.all_to_all(
+                jnp.stack(jnp.split(values, lax.axis_size(("seqa", "seqb")), axis=1)),
+                ("seqa", "seqb"),
+                0,
+                0,
+            ),
+            axis=0,
+        ),
     )
     attend_all = jax.vmap(attend_head, in_axes=(1, 1, 1, None, None, None), out_axes=1)
     result = attend_all(query_full, key_full, value_full, doc_bounds, q_gain, k_gain)

time: 52 us -> 52.2 us (level)
    unnamed x25 -> x31, local copies, waits for them, and re-layouts: 4.6 us -> 4.65 us
  transfers between devices with their start and end apart: 3 -> 3, of which waited for: 2 -> 2; matrix products, arithmetic and copies ran while one was open for 19% -> 20% of each run, Pallas kernels for 0% -> 0%
where the time goes in v1:
time: 52.2 us; the launch traced here: 51.6 us
  starting transfers between devices  16.8 us (32%)
  waiting for transfers between devices  10.6 us (20%)
  blocking collectives  9.06 us (17%)
  other arithmetic  7.48 us (14%)
  local copies, waits for them, and re-layouts  6.98 us (13%)
  matrix products  0.54 us (1%)
    all_to_all x1, blocking collectives, body(): lax.all_to_all(for_sending(result), ('seqa', 'seqb'), split_axis=0, conca...  9.06 us
    all_to_all x1, starting transfers between devices, body(): lax.all_to_all(queries, ('seqa', 'seqb'), split_axis=1, concat_axis=0, ti...  7.41 us
    all_to_all x1, waiting for transfers between devices, body(): lax.all_to_all(keys, ('seqa', 'seqb'), split_axis=1, concat_axis=0, tiled...  6.22 us
    all_to_all x1, starting transfers between devices, body(): lax.all_to_all(keys, ('seqa', 'seqb'), split_axis=1, concat_axis=0, tiled...  6 us
    unnamed x31, local copies, waits for them, and re-layouts  4.65 us
    gather x2, other arithmetic, attend_head(): positions = places - doc_bounds[doc]  4.39 us
    all_to_all x1, waiting for transfers between devices, body(): lax.all_to_all(jnp.stack(jnp.split(values, lax.axis_size(('seqa', 'seqb')...  4.37 us
    all_to_all x1, starting transfers between devices, body(): lax.all_to_all(jnp.stack(jnp.split(values, lax.axis_size(('seqa', 'seqb')...  3.34 us
  transfers between devices with their start and end apart: 3, of which 2 were waited for; matrix products, arithmetic and copies ran while one was open for 20% of the time, Pallas kernels for 0%

profile of v1, /device:TPU:0, one launch (start us, length us, event | category | flops | bytes accessed | tf_op | source)
XLA Modules:
  0.0 51.6 jit_solution(15404405116002688660)
XLA Ops:
  0.0 0.8 %copy.97 = bf16[32,8,64]{2,0,1:T(8,128)(2,1)S(1)} copy(bf16[32,8,64]{2,1,0:T(8,128)(2,1)} %param.6) | data formatting | bytes 65536 | tf_op args[0]
  0.9 0.7 %reshape.436 = bf16[8,2,1024]{2,1,0:T(2,128)(2,1)} reshape(bf16[8,32,64]{2,1,0:T(8,128)(2,1)S(1)} %bitcast.95) | data formatting | bytes 65536
  1.6 7.4 %all-to-all-start = ((bf16[8,2,1024]{2,1,0:T(2,128)(2,1)}), bf16[8,2,1024]{2,1,0:T(2,128)(2,1)S(1)}, u32[]{:S(2)}, u32[]{:S(2)}) async-start(bf16[8,2,1024]{2,1,0:T(2,128)(2,1)} %reshape.436), calls=%async_computation | async-start | bytes 65536 | tf_op jit(solution)/shard_map/all_to_all | solution.py:64
  9.0 0.7 %fusion.36 = (s32[1]{0:T(128)}, s32[1]{0:T(128)}, s32[1]{0:T(128)}, s32[1]{0:T(128)}, s32[1]{0:T(128)}, /*index=5*/s32[1]{0:T(128)}, s32[1]{0:T(128)}, s32[1]{0:T(128)}, s32[1]{0:T(128)}) fusion(s32[9]{0:T(128)S(1)} %copy-done.2), kind=kLoop, calls=%fused_computation.78 | loop fusion | bytes 72 | tf_op jit(solution)/shard_map/vmap()/gather | solution.py:37
  9.9 0.7 %reshape.438 = bf16[8,2,1024]{2,1,0:T(2,128)(2,1)} reshape(bf16[8,32,64]{2,1,0:T(8,128)(2,1)S(1)} %bitcast.96) | data formatting | bytes 65536
  10.6 0.1 copy-done
  10.7 0.1 fusion.35
  11.0 0.7 %reshape.434 = bf16[8,2,1024]{2,1,0:T(2,128)(2,1)} reshape(bf16[8,1,32,64]{3,2,1,0:T(8,128)(2,1)S(1)} %bitcast.97) | data formatting | bytes 65536
  11.7 4.4 %compare_select_fusion.1 = s32[256,1]{0,1:T(1,128)S(1)} fusion(s32[]{:T(128)} %bitcast.7, s32[]{:T(128)} %bitcast.8, s32[]{:T(128)} %bitcast.9, s32[]{:T(128)} %bitcast.10, s32[]{:T(128)} %bitcast.11, s32[]{:T(128)} %bitcast.13, s32[]{:T(128)} %bitcast.12, s32[256,1]{0,1:T(1,128)S(1)} %bitcast.100), kind=kLoop, calls=%fused_computation.66 | loop fusion | flops 3840 | bytes 2076 | tf_op jit(solution)/shard_map/vmap()/gather | solution.py:37
  16.1 1.2 %fusion.32 = f32[256]{0:T(256)S(1)} fusion(pred[256]{0:T(512)(128)(4,1)S(1)} %get-tuple-element.22, pred[256]{0:T(512)(128)(4,1)S(1)} %get-tuple-element.21, s32[256]{0:T(256)S(1)} %bitcast.101, s32[]{:T(128)} %bitcast.5, s32[]{:T(128)} %bitcast.6), kind=kLoop, calls=%fused_computation.73 | loop fusion | flops 1024 | bytes 2568 | tf_op jit(solution)/shard_map/vmap()/convert_element_type | solution.py:20
  17.3 6.0 %all-to-all-start.1 = ((bf16[8,2,1024]{2,1,0:T(2,128)(2,1)}), bf16[8,2,1024]{2,1,0:T(2,128)(2,1)S(1)}, u32[]{:S(2)}, u32[]{:S(2)}) async-start(bf16[8,2,1024]{2,1,0:T(2,128)(2,1)} %reshape.438), calls=%async_computation.1 | async-start | bytes 65536 | tf_op jit(solution)/shard_map/all_to_all | solution.py:65
  23.3 0.1 reshape.437
  23.4 0.1 multiply_reduce_fusion.1
  23.8 6.2 %all-to-all-done.1 = bf16[8,2,1024]{2,1,0:T(2,128)(2,1)S(1)} async-done(((bf16[8,2,1024]{2,1,0:T(2,128)(2,1)}), bf16[8,2,1024]{2,1,0:T(2,128)(2,1)S(1)}, u32[]{:S(2)}, u32[]{:S(2)}) %all-to-all-start.1) | async-done | bytes 32800 | tf_op jit(solution)/shard_map/all_to_all | solution.py:65
  30.0 3.3 %all-to-all-start.2 = ((bf16[8,2,1024]{2,1,0:T(2,128)(2,1)}), bf16[8,2,1024]{2,1,0:T(2,128)(2,1)S(1)}, u32[]{:S(2)}, u32[]{:S(2)}) async-start(bf16[8,2,1024]{2,1,0:T(2,128)(2,1)} %reshape.434), calls=%async_computation.2 | async-start | bytes 65536 | tf_op jit(solution)/shard_map/all_to_all | solution.py:67
  33.4 0.1 reshape.439
  33.5 0.1 multiply_reduce_fusion
  33.8 0.6 %copy-done.3 = f32[64]{0:T(128)S(1)} copy-done((f32[64]{0:T(128)S(1)}, f32[64]{0:T(128)}, u32[]{:S(2)}) %copy-start.3) | copy-done | bytes 280
  34.4 0.1 fusion.20
  34.6 0.6 %fusion.29 = (bf16[256,32]{1,0:T(8,128)(2,1)S(1)}, bf16[256,32]{1,0:T(8,128)(2,1)S(1)}, bf16[256,32]{1,0:T(8,128)(2,1)S(1)}, bf16[256,32]{1,0:T(8,128)(2,1)S(1)}) fusion(f32[1,256,64]{2,1,0:T(8,128)S(1)} %get-tuple-element.59, f32[32]{0:T(128)S(1)} %multiply_exponential_fusion, f32[256]{0:T(256)S(1)} %fusion.32, f32[1,256,64]{2,1,0:T(8,128)S(1)} %get-tuple-element.60), kind=kLoop, calls=%fused_computation.40 | loop fusion | flops 139264 | bytes 197760 | tf_op jit(solution)/shard_map/vmap()/concatenate | solution.py:25
  35.2 0.3 fusion.37
  35.5 0.1 fusion.11
  35.6 4.4 %all-to-all-done.2 = bf16[8,2,1024]{2,1,0:T(2,128)(2,1)S(1)} async-done(((bf16[8,2,1024]{2,1,0:T(2,128)(2,1)}), bf16[8,2,1024]{2,1,0:T(2,128)(2,1)S(1)}, u32[]{:S(2)}, u32[]{:S(2)}) %all-to-all-start.2) | async-done | bytes 32800 | tf_op jit(solution)/shard_map/all_to_all | solution.py:67
  40.0 0.1 reshape.435
  40.1 0.2 fusion.1
  40.4 0.5 broadcast.313
  40.9 0.7 %reduce.16 = bf16[256,64]{0,1:T(8,128)(2,1)S(1)} reduce(bf16[256,1,64]{0,2,1:T(8,128)(2,1)S(1)} %fusion.1, bf16[]{:T(256)} %broadcast.313), dimensions={1}, to_apply=%copy.57.reduce_sub_computation | reduce | bytes 65538 | tf_op jit(solution)/shard_map/vmap()/transpose;vmap()/reshape;vmap()/transpose | solution.py:77
  41.5 0.1 copy.98
  41.6 0.1 reshape.440
  41.8 9.1 %all_to_all.41 = bf16[8,2,1024]{2,1,0:T(2,128)(2,1)S(1)} all-to-all(bf16[8,2,1024]{2,1,0:T(2,128)(2,1)S(1)} %reshape.440), channel_id=1, replica_groups=mesh['seqa'=4,'seqb'=2,'dp'=4] {'seqa','seqb'}, dimensions={0} | all-to-all | bytes 65536 | tf_op jit(solution)/shard_map/all_to_all | solution.py:80
  50.8 0.1 reshape.441
  51.0 0.7 %copy.58 = bf16[32,8,64]{2,1,0:T(8,128)(2,1)} copy(bf16[32,8,64]{2,0,1:T(8,128)(2,1)S(1)} %bitcast.94) | data formatting | bytes 65536 | tf_op jit(solution)/shard_map/all_to_all | solution.py:80
  (31 shorter events, 0.8 us)
Async XLA Ops:
  0.9 8.1 %copy-start.2 = (s32[9]{0:T(128)S(1)}, s32[9]{0:T(128)}, u32[]{:S(2)}) copy-start(s32[9]{0:T(128)} %param.9) | copy-start | bytes 112
  1.6 8.3 %copy-start.1 = (bf16[32,8,64]{2,1,0:T(8,128)(2,1)S(1)}, bf16[32,8,64]{2,1,0:T(8,128)(2,1)}, u32[]{:S(2)}) copy-start(bf16[32,8,64]{2,1,0:T(8,128)(2,1)} %param.7) | copy-start | bytes 98308
  1.6 15.7 %all-to-all-start = ((bf16[8,2,1024]{2,1,0:T(2,128)(2,1)}), bf16[8,2,1024]{2,1,0:T(2,128)(2,1)S(1)}, u32[]{:S(2)}, u32[]{:S(2)}) async-start(bf16[8,2,1024]{2,1,0:T(2,128)(2,1)} %reshape.436), calls=%async_computation | async-start | bytes 65536 | tf_op jit(solution)/shard_map/all_to_all | solution.py:64
  9.9 0.8 %copy-start = (bf16[32,8,64]{2,1,0:T(8,128)(2,1)S(1)}, bf16[32,8,64]{2,1,0:T(8,128)(2,1)}, u32[]{:S(2)}) copy-start(bf16[32,8,64]{2,1,0:T(8,128)(2,1)} %param.8) | copy-start | bytes 98308
  17.3 12.7 %all-to-all-start.1 = ((bf16[8,2,1024]{2,1,0:T(2,128)(2,1)}), bf16[8,2,1024]{2,1,0:T(2,128)(2,1)S(1)}, u32[]{:S(2)}, u32[]{:S(2)}) async-start(bf16[8,2,1024]{2,1,0:T(2,128)(2,1)} %reshape.438), calls=%async_computation.1 | async-start | bytes 65536 | tf_op jit(solution)/shard_map/all_to_all | solution.py:65
  30.0 10.0 %all-to-all-start.2 = ((bf16[8,2,1024]{2,1,0:T(2,128)(2,1)}), bf16[8,2,1024]{2,1,0:T(2,128)(2,1)S(1)}, u32[]{:S(2)}, u32[]{:S(2)}) async-start(bf16[8,2,1024]{2,1,0:T(2,128)(2,1)} %reshape.434), calls=%async_computation.2 | async-start | bytes 65536 | tf_op jit(solution)/shard_map/all_to_all | solution.py:67
  33.8 0.7 %copy-start.3 = (f32[64]{0:T(128)S(1)}, f32[64]{0:T(128)}, u32[]{:S(2)}) copy-start(f32[64]{0:T(128)} %param.11) | copy-start | bytes 772
  33.8 0.7 %copy-start.4 = (f32[64]{0:T(128)S(1)}, f32[64]{0:T(128)}, u32[]{:S(2)}) copy-start(f32[64]{0:T(128)} %param.10) | copy-start | bytes 772
